TPU v7x, 32 devices: a 4x4x1 block of a 4x4x8 slice. The times are simulated.
32 devices in a mesh: rep: 2 (over z, core), dp: 16 (over x, y).
Axes of the slice: x: 4, y: 4, z: 1, core: 2. Of those that a mesh axis runs over, the one named last changes fastest.
The devices are a block of a 4x4x8 slice.
Arguments:
- g_w_gate: bfloat16 [32, 2, 896, 2304], P(('rep', 'dp')), parts along dimension 0
- g_w_up: bfloat16 [32, 2, 896, 2304], P(('rep', 'dp')), parts along dimension 0
- g_w_down: bfloat16 [32, 2, 2304, 896], P(('rep', 'dp')), parts along dimension 0
- w_gate: bfloat16 [2, 896, 2304], replicated
- w_up: bfloat16 [2, 896, 2304], replicated
- w_down: bfloat16 [2, 2304, 896], replicated
- m_w_gate: float32 [2, 896, 2304], P(None, 'dp')
- m_w_up: float32 [2, 896, 2304], P(None, 'dp')
- m_w_down: float32 [2, 2304, 896], P(None, 'dp')
- v_w_gate: float32 [2, 896, 2304], P(None, 'dp')
- v_w_up: float32 [2, 896, 2304], P(None, 'dp')
- v_w_down: float32 [2, 2304, 896], P(None, 'dp')
Outputs:
- output 1: bfloat16 [4, 896, 2304], P('rep'), parts along dimension 0
- output 2: bfloat16 [4, 896, 2304], P('rep'), parts along dimension 0
- output 3: bfloat16 [4, 2304, 896], P('rep'), parts along dimension 0
- output 4: float32 [4, 896, 2304], P('rep', 'dp'), parts along dimension 0
- output 5: float32 [4, 896, 2304], P('rep', 'dp'), parts along dimension 0
- output 6: float32 [4, 2304, 896], P('rep', 'dp'), parts along dimension 0
- output 7: float32 [4, 896, 2304], P('rep', 'dp'), parts along dimension 0
- output 8: float32 [4, 896, 2304], P('rep', 'dp'), parts along dimension 0
- output 9: float32 [4, 2304, 896], P('rep', 'dp'), parts along dimension 0
There are 2 independent parts. A program takes and returns all parts, laid end to end along the dimension named above; an argument that names none is the same for every part.
All inputs are finite; a program needn't handle non-finite values.
Results may differ from a plain program's by a relative error of at most 0.022.
Values are sent between devices in bfloat16 or wider.
A program may use at most 768 MiB of HBM per device.

v0:
```python
import jax
import jax.numpy as jnp
from jax import lax
from jax.sharding import PartitionSpec as P


def adamw(w, m, v, g):
    m = 0.9 * m + 0.1 * g
    v = 0.95 * v + 0.05 * g * g
    step = m * lax.rsqrt(v + 1e-8) + 0.1 * w
    return (w - 0.02 * step).astype(jnp.bfloat16), m, v


def clipped(gradients, sum_of_squares, count):
    factor = jnp.minimum(1.0, 0.5 * lax.rsqrt(sum_of_squares / count + 1e-30))
    return [g * factor for g in gradients]


def solution(mesh):
    def step(*arrays):
        terms, weights, m, v = (arrays[i : i + 3] for i in (0, 3, 6, 9))
        gradients = [lax.psum_scatter(t[0], "dp", scatter_dimension=1, tiled=True).astype(jnp.float32) for t in terms]
        squares = lax.psum(sum(jnp.sum(g * g) for g in gradients), "dp")
        gradients = clipped(gradients, squares, lax.psum(1, "dp") * sum(g.size for g in gradients))
        me = lax.axis_index("dp")
        own = [lax.dynamic_slice_in_dim(w, me * one.shape[1], one.shape[1], 1).astype(jnp.float32) for w, one in zip(weights, m, strict=True)]
        new = [adamw(w, m, v, g) for w, m, v, g in zip(own, m, v, gradients, strict=True)]
        whole = [lax.all_gather(one[0], "dp", axis=1, tiled=True) for one in new]
        return (*whole, *(one[1] for one in new), *(one[2] for one in new))

    all_of, cut = P(None, None, None), P(None, "dp", None)
    return jax.shard_map(
        step,
        mesh=mesh,
        in_specs=(P(("rep", "dp"), None, None, None),) * 3 + (all_of,) * 3 + (cut,) * 6,
        out_specs=(P("rep", None, None),) * 3 + (P("rep", "dp", None),) * 6,
        check_vma=False,
    )
```

profile of v0, /device:TPU:96, one launch (start us, length us, event | category | flops | bytes accessed | tf_op | source)
XLA Modules:
  0.0 575.6 jit_solution(2260729458088868210)
XLA Ops:
  7.2 0.1 all-reduce.5.cloned.1.call-start
  7.3 0.7 all-reduce.5.cloned.1.call-update
  8.0 0.0 copy-start.3
  8.0 0.0 copy-start.1
  8.0 0.0 copy-start.2
  8.0 0.1 reduce-scatter.4.cloned.1.call-start
  8.1 0.7 reduce-scatter.4.cloned.1.call-update
  8.8 0.1 all-gather.4.cloned.1.call-start
  8.9 0.0 copy-done.3
  8.9 0.6 dynamic-slice
  10.2 211.0 %all-reduce.5.cloned.1.call-done = (bf16[2,896,2304]{2,1,0:T(8,128)(2,1)}, bf16[2,896,2304]{2,1,0:T(8,128)(2,1)}) async-done(((bf16[2,896,2304]{2,1,0:T(8,128)(2,1)}, bf16[2,896,2304]{2,1,0:T(8,128)(2,1)}), (bf16[2,896,2304]{2,1,0:T(8,128)(2,1)}, bf16[2,896,2304]{2,1,0:T(8,128)(2,1)})) %all-reduce.5.cloned.1.call-update) | async-done | bytes 16515088
  221.1 2.1 fusion.9
  224.5 82.9 %reduce-scatter.4.cloned.1.call-done = bf16[2,144,896]{2,1,0:T(8,128)(2,1)} async-done(((bf16[2,2304,896]{2,1,0:T(8,128)(2,1)}), bf16[2,144,896]{2,1,0:T(8,128)(2,1)}) %reduce-scatter.4.cloned.1.call-update) | async-done | bytes 516112 | tf_op jit(solution)/shard_map/reduce_scatter | solution.py:22
  307.3 0.0 copy-start
  307.3 2.0 fusion.11
  310.0 38.7 %psum.7 = f32[]{:T(128)} all-reduce(f32[]{:T(128)S(6)} %add.65), channel_id=1, replica_groups=mesh['rep'=2,'dp'=16] {'dp'}, use_global_device_ids=true, to_apply=%region_6.0 | all-reduce | flops 1 | bytes 8 | tf_op jit(solution)/shard_map/psum | solution.py:23
  349.3 0.0 copy-done.1
  349.3 0.0 copy-done.2
  349.3 3.0 fusion.8
  352.3 0.1 all-gather.4.cloned.1.call-update
  352.4 0.1 all-gather.6.cloned.1.call-start
  352.5 3.6 fusion.14
  356.1 0.1 all-gather.6.cloned.1.call-update
  356.1 0.1 all-gather.8.cloned.1.call-start
  356.2 0.0 copy-done
  356.2 3.4 fusion.17
  359.7 0.1 all-gather.8.cloned.1.call-update
  359.7 53.5 %all-gather.4.cloned.1.call-done = bf16[2,896,2304]{2,1,0:T(8,128)(2,1)} async-done(((bf16[2,56,2304]{2,1,0:T(8,128)(2,1)}), bf16[2,896,2304]{2,1,0:T(8,128)(2,1)}) %all-gather.4.cloned.1.call-update) | async-done | bytes 8257552 | tf_op jit(solution)/shard_map/all_gather | solution.py:28
  413.3 67.0 %all-gather.6.cloned.1.call-done = bf16[2,896,2304]{2,1,0:T(8,128)(2,1)} async-done(((bf16[2,56,2304]{2,1,0:T(8,128)(2,1)}), bf16[2,896,2304]{2,1,0:T(8,128)(2,1)}) %all-gather.6.cloned.1.call-update) | async-done | bytes 8257552 | tf_op jit(solution)/shard_map/all_gather | solution.py:28
  480.2 67.0 %all-gather.8.cloned.1.call-done = bf16[2,2304,896]{2,1,0:T(8,128)(2,1)} async-done(((bf16[2,144,896]{2,1,0:T(8,128)(2,1)}), bf16[2,2304,896]{2,1,0:T(8,128)(2,1)}) %all-gather.8.cloned.1.call-update) | async-done | bytes 8257552 | tf_op jit(solution)/shard_map/all_gather | solution.py:28
  547.2 7.2 %copy.32 = bf16[2,896,2304]{2,1,0:T(8,128)(2,1)} copy(bf16[2,896,2304]{2,1,0:T(8,128)(2,1)} %all-gather.4.cloned.1.call-done) | data formatting | bytes 16515072
  554.4 7.2 %copy.33 = bf16[2,896,2304]{2,1,0:T(8,128)(2,1)} copy(bf16[2,896,2304]{2,1,0:T(8,128)(2,1)} %all-gather.6.cloned.1.call-done) | data formatting | bytes 16515072
  561.7 7.3 %copy.34 = bf16[2,2304,896]{2,1,0:T(8,128)(2,1)} copy(bf16[2,2304,896]{2,1,0:T(8,128)(2,1)} %all-gather.8.cloned.1.call-done) | data formatting | bytes 16515072
Async XLA Ops:
  7.2 213.9 %all-reduce.5.cloned.1.call-start = ((), (), s32[]{:S(2)}) async-start(), calls=%async_computation.5 | async-start | bytes 33030144
  8.0 0.9 copy-start.3
  8.0 341.3 %copy-start.1 = (f32[2,56,2304]{2,1,0:T(8,128)S(1)}, f32[2,56,2304]{2,1,0:T(8,128)}, u32[]{:S(2)}) copy-start(f32[2,56,2304]{2,1,0:T(8,128)} %param.21) | copy-start | bytes 3096580
  8.0 341.3 %copy-start.2 = (f32[2,56,2304]{2,1,0:T(8,128)S(1)}, f32[2,56,2304]{2,1,0:T(8,128)}, u32[]{:S(2)}) copy-start(f32[2,56,2304]{2,1,0:T(8,128)} %param.18) | copy-start | bytes 3096580
  8.0 299.3 %reduce-scatter.4.cloned.1.call-start = ((), (), s32[]{:S(2)}) async-start(), calls=%async_computation.1 | async-start | bytes 8773632 | tf_op jit(solution)/shard_map/reduce_scatter | solution.py:22
  8.8 404.4 %all-gather.4.cloned.1.call-start = ((), (), s32[]{:S(2)}) async-start(), calls=%async_computation.2 | async-start | bytes 8773632 | tf_op jit(solution)/shard_map/all_gather | solution.py:28
  307.3 48.9 %copy-start = (bf16[2,144,896]{2,1,0:T(8,128)(2,1)S(1)}, bf16[2,144,896]{2,1,0:T(8,128)(2,1)}, u32[]{:S(2)}) copy-start(bf16[2,144,896]{2,1,0:T(8,128)(2,1)} %reduce-scatter.4.cloned.1.call-done) | copy-start | bytes 1548292
  352.4 127.8 %all-gather.6.cloned.1.call-start = ((), (), s32[]{:S(2)}) async-start(), calls=%async_computation.3 | async-start | bytes 8773632 | tf_op jit(solution)/shard_map/all_gather | solution.py:28
  356.1 191.1 %all-gather.8.cloned.1.call-start = ((), (), s32[]{:S(2)}) async-start(), calls=%async_computation.4 | async-start | bytes 8773632 | tf_op jit(solution)/shard_map/all_gather | solution.py:28
Sparse Core Ops, SparseCore 0:
  12.1 208.9 all-reduce.4
  224.4 82.8 reduce-scatter.3
  352.5 60.6 all-gather.3
  415.7 64.4 all-gather.5
  482.7 64.4 all-gather.7
where the time goes:
time: 577 us; the launch traced here: 576 us
  waiting for transfers between devices  483 us (84%)
  blocking collectives  38.7 us (7%)
  local copies, waits for them, and re-layouts  22.4 us (4%)
  between operations  17.2 us (3%)
  other arithmetic  14.1 us (2%)
    unnamed x6, waiting for transfers between devices  213 us
    all_gather x3, waiting for transfers between devices, step(): whole = [lax.all_gather(one[0], 'dp', axis=1, tiled=True) for one in new]  187 us
    reduce_scatter x1, waiting for transfers between devices, step(): lax.psum_scatter(t[0], 'dp', scatter_dimension=1, tiled=True)  82.9 us
    psum x1, blocking collectives, step(): squares = lax.psum(sum((jnp.sum(g * g) for g in gradients)), 'dp')  38.7 us
    unnamed x12, local copies, waits for them, and re-layouts  22.4 us
  transfers between devices with their start and end apart: 5, of which 5 were waited for; matrix products, arithmetic and copies ran while one was open for 2% of the time, Pallas kernels for 0%

commit v1 on v0

v1 whole, which is shorter than its diff:
```python
import functools
import heapq
import math

import jax
import jax.numpy as jnp
from jax import lax
from jax.experimental import pallas as pl
from jax.experimental.pallas import tpu as pltpu
from jax.sharding import PartitionSpec as P

F32, BF16 = jnp.float32, jnp.bfloat16
MESH = pl.DeviceIdType.MESH
SIGN = (1, -1)


def gather_order(side):
    free = {(a, d): 0.0 for a in range(2) for d in range(2)}
    size = (2.0, 1.0)
    events, start, order, count = [], [], [], 0

    def enqueue(now, link, piece, d, first):
        nonlocal count
        c, r1, r2, h, p = piece
        free[link] = max(free[link], now) + size[p]
        there = (c, (r1 - SIGN[d]) % side, r2, h, p) if first else (c, r1, (r2 - SIGN[d]) % side, h, p)
        count += 1
        heapq.heappush(events, (free[link] + 1.0, count, there, link))

    def sends(piece, link):
        c, r1, r2, h, p = piece
        axes = (1, 0) if c == 0 else (0, 1)
        out = []
        if r1 == 0 and r2 == 0:
            out += [(axes[0], d, True) for d in range(2)]
        if r2 == 0:
            if r1 != 0 and r1 != 2 and link[1] == h:
                out.append((axes[0], h, True))
            out += [(axes[1], d, False) for d in range(2)]
        elif r2 != 2 and link[1] == h:
            out.append((axes[1], h, False))
        return out

    now = 0.0
    for p in (1, 0):
        for h in range(2):
            for c in range(2):
                piece = (c, 0, 0, h, p)
                todo = sends(piece, None)
                start.append((piece, todo))
                for a, d, first in todo:
                    enqueue(now, (a, d), piece, d, first)
                now += 0.1
    while events:
        now, _, piece, link = heapq.heappop(events)
        todo = sends(piece, link)
        order.append((piece, todo))
        for a, d, first in todo:
            enqueue(now, (a, d), piece, d, first)
    return start, order


def columns(shape):
    return 384 if shape[-1] % 384 == 0 else 128


def loop(shape, body, carry=0):
    width = columns(shape)

    def step(i, carry):
        return body(pl.ds(pl.multiple_of(i * width, width), width), carry)

    return lax.fori_loop(0, shape[-1] // width, step, carry)


def squares(x):
    total = None
    for i in range(0, x.shape[0], 8):
        for j in range(0, x.shape[1], 128):
            one = x[i : i + 8, j : j + 128]
            total = one * one if total is None else total + one * one
    return total


def kernel(n, side, count, ga, gb, gd, wa, wb, wd, ma, mb, md, va, vb, vd,
           oa, ob, od, oma, omb, omd, ova, ovb, ovd,
           fwd_big, fwd_small, own_big, own_small, acc_big, acc_small, w_big, w_small, part,
           load_sem, send_big, send_small, recv, part_send, part_recv):
    me = lax.axis_index("dp")
    at = (me // side, me % side)

    def block(c, q1, q2):
        return q1 * side + q2 if c == 0 else q2 * side + q1

    def neighbour(axis, d):
        moved = lax.rem(at[axis] + SIGN[d] + side, side)
        return moved * side + at[1] if axis == 0 else at[0] * side + moved

    def near(p, steps):
        return lax.rem(p + steps + side, side)

    g_big, out_big = (ga, gb), (oa, ob)

    loads = {}

    def load(key, index, src, dst):
        copy = pltpu.make_async_copy(src, dst, load_sem.at[index])
        copy.start()
        loads[key] = copy

    def rows(ref, c, q1):
        return ref.at[c, q1] if c == 0 else ref.at[c, :, q1]

    index = 0
    for d in range(2):
        for c in range(2):
            q1 = near(at[c], SIGN[d])
            load(("fwd", c, d, 0), index, rows(g_big[d], c, q1), fwd_big.at[c, d])
            load(("fwd", c, d, 1), index + 1, (gd.at[c, q1, :, d] if c == 0 else gd.at[c, :, q1, d]), fwd_small.at[c, d])
            index += 2
    for h in range(2):
        for c in range(2):
            load(("own", c, h, 0), index, rows(g_big[h], c, at[c]), own_big.at[c, h])
            load(("own", c, h, 1), index + 1, (gd.at[c, at[c], :, h] if c == 0 else gd.at[c, :, at[c], h]), own_small.at[c, h])
            index += 2

    barrier = pltpu.get_barrier_semaphore()
    for i in range(1, n):
        pl.semaphore_signal(barrier, inc=1, device_id={"dp": lax.rem(me + i, n)}, device_id_type=MESH)
    pl.semaphore_wait(barrier, n - 1)

    def slot(c, d, p, s):
        return out_big[d].at[c * n + s] if p == 0 else od.at[c * n + s, d]

    def send(src, dst, axis, d, p, sem):
        sems = send_big if p == 0 else send_small
        link = 2 * axis + d
        pltpu.make_async_remote_copy(
            src_ref=src, dst_ref=dst, send_sem=sems.at[link if p == 0 else axis], recv_sem=sem,
            device_id={"dp": neighbour(axis, d)}, device_id_type=MESH).start()

    def arrived(ref, sem):
        pltpu.make_async_copy(ref, ref, sem).wait()

    def to_slot(src, c, d, axis, p, s):
        send(src, slot(c, d, p, s), axis, d, p, recv.at[c, d, p, s])

    def wait_slot(c, d, p, s):
        arrived(slot(c, d, p, s), recv.at[c, d, p, s])

    def term_ref(c, h, p, q1, q2):
        i, j = (q1, q2) if c == 0 else (q2, q1)
        return g_big[h].at[c, i, j] if p == 0 else gd.at[c, i, j, h]

    ks = (2, 1, -1, 0)

    def step1(c, d, k):
        for p in range(2):
            to_slot(term_ref(c, d, p, near(at[c], 2), near(at[1 - c], ks[k])), c, d, c, p, k)

    def step2(c, d, k):
        for p in range(2):
            to_slot(term_ref(c, 1 - d, p, near(at[c], SIGN[d]), near(at[1 - c], ks[k])), c, d, c, p, 4 + k)

    for k in range(4):
        for d in range(2):
            for c in range(2):
                step1(c, d, k)
    for k in range(2):
        for d in range(2):
            for c in range(2):
                step2(c, d, k)

    own = (own_big, own_small)
    fwd = (fwd_big, fwd_small)
    acc = (acc_big, acc_small)
    shapes = (own_big.shape[-2:], own_small.shape[-2:])

    for copy in list(loads.values())[: 8]:
        copy.wait()

    def add_fwd(c, d, p, s, src):
        dst = slot(c, d, p, s)

        def body(cols, _):
            dst[:, cols] = (dst[:, cols].astype(F32) + src[:, cols].astype(F32)).astype(BF16)
            return 0

        loop(shapes[p], body)

    for k in range(4):
        for d in range(2):
            for c in range(2):
                for p in range(2):
                    wait_slot(c, d, p, k)
                    add_fwd(c, d, p, k, fwd[p].at[c, d, near(at[1 - c], ks[k])])
                    to_slot(slot(c, d, p, k), c, d, c, p, 8 + k)
                if k < 2:
                    step2(c, d, k + 2)

    for copy in list(loads.values())[8:]:
        copy.wait()

    updates = {}
    for h, (m, v, w, om, ov) in enumerate(((ma, va, wa, oma, ova), (mb, vb, wb, omb, ovb))):
        load(("m", h, 0), index, m, om)
        load(("v", h, 0), index + 1, v, ov)
        load(("w", h, 0), index + 2, w.at[:, me], w_big.at[h])
        index += 3
    load(("m", 1), index, md, omd)
    load(("v", 1), index + 1, vd, ovd)
    load(("w", 1), index + 2, wd.at[:, me], w_small)

    for k in range(4):
        for h in range(2):
            for c in range(2):
                q2 = near(at[1 - c], ks[k])
                for p in range(2):
                    wait_slot(c, h, p, 8 + k)
                    wait_slot(c, 1 - h, p, 4 + k)
                    mine, one, two = own[p].at[c, h, q2], slot(c, h, p, 8 + k), slot(c, 1 - h, p, 4 + k)
                    dst = mine if k < 3 else acc[p].at[c, h]

                    def body(cols, _, mine=mine, one=one, two=two, dst=dst):
                        x = mine[:, cols].astype(F32) + one[:, cols].astype(F32) + two[:, cols].astype(F32)
                        dst[:, cols] = x.astype(dst.dtype)
                        return 0

                    loop(shapes[p], body)
                    if k == 0:
                        to_slot(mine, c, h, 1 - c, p, 12)
                    if (k == 1 and h == 1) or (k == 2 and h == 0):
                        to_slot(mine, c, 1 - h, 1 - c, p, 13)

    for p in range(2):
        for d in range(2):
            for c in range(2):
                wait_slot(c, d, p, 12)
                add_fwd(c, d, p, 12, own[p].at[c, d, near(at[1 - c], SIGN[d])])
                to_slot(slot(c, d, p, 12), c, d, 1 - c, p, 14)

    total = jnp.zeros((8, 128), F32)
    for p in range(2):
        for h in range(2):
            for c in range(2):
                wait_slot(c, h, p, 14)
                wait_slot(c, 1 - h, p, 13)
                mine, one, two = acc[p].at[c, h], slot(c, h, p, 14), slot(c, 1 - h, p, 13)

                def body(cols, total, mine=mine, one=one, two=two):
                    x = mine[:, cols] + one[:, cols].astype(F32) + two[:, cols].astype(F32)
                    x = x.astype(BF16).astype(F32)
                    mine[:, cols] = x
                    return total + squares(x)

                total = loop(shapes[p], body, total)

    def wait_sends():
        many = n - 1
        for link in range(4):
            ref = oa.at[pl.ds(0, many)]
            pltpu.make_async_copy(ref, ref, send_big.at[link]).wait()
        for axis in range(2):
            ref = od.at[pl.ds(0, many)]
            pltpu.make_async_copy(ref, ref, send_small.at[axis]).wait()

    wait_sends()

    part[me] = total
    copies = []
    for i in range(1, n):
        to = lax.rem(me + i, n)
        copy = pltpu.make_async_remote_copy(
            src_ref=part.at[me], dst_ref=part.at[me], send_sem=part_send.at[i - 1], recv_sem=part_recv.at[i - 1],
            device_id={"dp": to}, device_id_type=MESH)
        copy.start()
        copies.append(copy)
    for copy in list(loads.values())[16:]:
        copy.wait()
    for i in range(1, n):
        back = lax.rem(me - i + n, n)
        arrived(part.at[back], part_recv.at[i - 1])
    total = part[0]
    for i in range(1, n):
        total = total + part[i]
    total = jnp.sum(total, keepdims=True)
    factor = jnp.minimum(1.0, 0.5 * lax.rsqrt(total / count + 1e-30))

    oms, ovs = (oma, omb), (ova, ovb)
    start, order = gather_order(side)

    def gathered(piece):
        c, r1, r2, h, p = piece
        q1, q2 = near(at[1 - c], r1), near(at[c], r2)
        b = q2 * side + q1 if c == 0 else q1 * side + q2
        return (out_big[h].at[c * n + b] if p == 0 else od.at[c * n + b, h]), recv.at[c, h, p, b]

    def pass_on(piece, todo):
        ref, sem = gathered(piece)
        for a, d, _ in todo:
            send(ref, ref, a, d, piece[-1], sem)

    for piece, todo in start:
        c, _, _, h, p = piece
        g = acc[p].at[c, h]
        m, v = (oms[h].at[c], ovs[h].at[c]) if p == 0 else (omd.at[c, h], ovd.at[c, h])
        w = w_big.at[h, c] if p == 0 else w_small.at[c, h]
        out, _ = gathered(piece)

        def body(cols, _, g=g, m=m, v=v, w=w, out=out):
            x = g[:, cols] * factor
            m1 = 0.9 * m[:, cols] + 0.1 * x
            v1 = 0.95 * v[:, cols] + 0.05 * x * x
            m[:, cols] = m1
            v[:, cols] = v1
            w1 = w[:, cols].astype(F32)
            out[:, cols] = (w1 - 0.02 * (m1 * lax.rsqrt(v1 + 1e-8) + 0.1 * w1)).astype(BF16)
            return 0

        loop(shapes[p], body)
        pass_on(piece, todo)
    for piece, todo in order:
        arrived(*gathered(piece))
        pass_on(piece, todo)
    wait_sends()
    for copy in copies:
        copy.wait_send()


def write_out(*refs):
    sem = refs[-1]
    copies = [pltpu.make_async_copy(refs[i], refs[9 + i], sem.at[i]) for i in range(9)]
    for copy in copies:
        copy.start()
    for copy in copies:
        copy.wait()


def solution(mesh):
    n = mesh.shape["dp"]
    side = math.isqrt(n)

    def step(*arrays):
        terms, weights, m, v = (arrays[i : i + 3] for i in (0, 3, 6, 9))
        layers, block_rows, wide = m[0].shape
        down_rows, narrow = m[2].shape[1] // 2, m[2].shape[2]
        big, small = (block_rows, wide), (down_rows, narrow)
        ins = [terms[0].reshape(layers, side, side, *big), terms[1].reshape(layers, side, side, *big),
               terms[2].reshape(layers, side, side, 2, *small),
               weights[0].reshape(layers, n, *big), weights[1].reshape(layers, n, *big), weights[2].reshape(layers, n, 2, *small)]
        for three in (m, v):
            ins += [three[0], three[1], three[2].reshape(layers, 2, *small)]
        outs = [((layers * n, *big), BF16)] * 2 + [((layers * n, 2, *small), BF16)]
        outs += ([((layers, *big), F32)] * 2 + [((layers, 2, *small), F32)]) * 2
        count = n * sum(one.size for one in m)
        res = pl.pallas_call(
            functools.partial(kernel, n, side, count),
            out_shape=[pltpu.VMEM(*one) for one in outs],
            in_specs=[pl.BlockSpec(memory_space=pl.ANY)] * 12,
            out_specs=[pl.BlockSpec(memory_space=pltpu.VMEM)] * 9,
            scratch_shapes=[
                pltpu.VMEM((layers, 2, side, *big), BF16),
                pltpu.VMEM((layers, 2, side, *small), BF16),
                pltpu.VMEM((layers, 2, side, *big), BF16),
                pltpu.VMEM((layers, 2, side, *small), BF16),
                pltpu.VMEM((layers, 2, *big), F32),
                pltpu.VMEM((layers, 2, *small), F32),
                pltpu.VMEM((2, layers, *big), BF16),
                pltpu.VMEM((layers, 2, *small), BF16),
                pltpu.VMEM((n, 8, 128), F32),
                pltpu.SemaphoreType.DMA((25,)),
                pltpu.SemaphoreType.DMA((4,)),
                pltpu.SemaphoreType.DMA((2,)),
                pltpu.SemaphoreType.DMA((layers, 2, 2, n)),
                pltpu.SemaphoreType.DMA((n - 1,)),
                pltpu.SemaphoreType.DMA((n - 1,)),
            ],
            compiler_params=pltpu.CompilerParams(collective_id=0, has_side_effects=True, vmem_limit_bytes=24 * 2**20),
        )(*ins)
        res = pl.pallas_call(
            write_out,
            out_shape=[jax.ShapeDtypeStruct(*one) for one in outs],
            in_specs=[pl.BlockSpec(memory_space=pltpu.VMEM)] * 9,
            out_specs=[pl.BlockSpec(memory_space=pl.ANY)] * 9,
            scratch_shapes=[pltpu.SemaphoreType.DMA((9,))],
            compiler_params=pltpu.CompilerParams(vmem_limit_bytes=2**20),
        )(*res)
        return tuple(r.reshape(layers, -1, r.shape[-1]) for r in res)

    all_of, cut = P(None, None, None), P(None, "dp", None)
    return jax.shard_map(
        step,
        mesh=mesh,
        in_specs=(P(("rep", "dp"), None, None, None),) * 3 + (all_of,) * 3 + (cut,) * 6,
        out_specs=(P("rep", None, None),) * 3 + (P("rep", "dp", None),) * 6,
        check_vma=False,
    )
```

time: 577 us -> 277 us (0.48)
  waiting for transfers between devices: 483 us -> 0 us
  Pallas kernels: 0 us -> 276 us
  blocking collectives: 38.7 us -> 0 us
  local copies, waits for them, and re-layouts: 22.4 us -> 0 us
  between operations: 17.2 us -> 0.65 us
  other arithmetic: 14.1 us -> 0 us
    pallas_call x0 -> x2, Pallas kernels: none -> 276 us  [the longest x1 266 us: step(): pl.pallas_call(functools.partial(kernel, n, side, count), out_shape=[pltp...]
    unnamed x6 -> x0, waiting for transfers between devices: 213 us -> none
    all_gather x3 -> x0, waiting for transfers between devices: 187 us -> none  [step(): whole = [lax.all_gather(one[0], 'dp', axis=1, tiled=True) for one in new]]
    reduce_scatter x1 -> x0, waiting for transfers between devices: 82.9 us -> none  [step(): lax.psum_scatter(t[0], 'dp', scatter_dimension=1, tiled=True)]
    psum x1 -> x0, blocking collectives: 38.7 us -> none  [step(): squares = lax.psum(sum((jnp.sum(g * g) for g in gradients)), 'dp')]
    unnamed x12 -> x0, local copies, waits for them, and re-layouts: 22.4 us -> none
    convert_element_type x3 -> x0, other arithmetic: 10 us -> none  [adamw(): return ((w - 0.02 * step).astype(jnp.bfloat16), m, v)]
  transfers between devices with their start and end apart: 5 -> 0, of which waited for: 5 -> 0; matrix products, arithmetic and copies ran while one was open for 2% -> 0% of each run, Pallas kernels for 0% -> 0%
where the time goes in v1:
time: 277 us
  Pallas kernels  276 us (100%)
    pallas_call x1, Pallas kernels, step(): pl.pallas_call(functools.partial(kernel, n, side, count), out_shape=[pltp...  266 us
    pallas_call x1, Pallas kernels, step(): pl.pallas_call(write_out, out_shape=[jax.ShapeDtypeStruct(*one) for one i...  10.3 us

profile of v1, /device:TPU:96, one launch (start us, length us, event | category | flops | bytes accessed | tf_op | source)
XLA Modules:
  0.0 276.7 jit_solution(15074047755054341436)
XLA Ops:
  0.6 265.7 %shard_map.187 = (bf16[32,56,2304]{2,1,0:T(8,128)(2,1)S(1)}, bf16[32,56,2304]{2,1,0:T(8,128)(2,1)S(1)}, bf16[32,2,72,896]{3,2,1,0:T(8,128)(2,1)S(1)}, f32[2,56,2...) custom-call(bf16[2,4,4,56,2304]{4,3,2,1,0:T(8,128)(2,1)} %bitcast.13, ...), custom_call_target="tpu_custom_call" | custom-call | tf_op jit(solution)/shard_map/pallas_call | solution.py:356
  266.4 10.3 %shard_map.188 = (bf16[32,56,2304]{2,1,0:T(8,128)(2,1)}, bf16[32,56,2304]{2,1,0:T(8,128)(2,1)}, bf16[32,2,72,896]{3,2,1,0:T(8,128)(2,1)}, f32[2,56,2304]{2,1,0:T...) custom-call(bf16[32,56,2304]{2,1,0:T(8,128)(2,1)S(1)} %get-tuple-ele, ...), custom_call_target="tpu_custom_call" | custom-call | tf_op jit(solution)/shard_map/pallas_call | solution.py:380

commit v2 on v1

--- a/solution.py
+++ b/solution.py
@@ -111,6 +111,54 @@
     def rows(ref, c, q1):
         return ref.at[c, q1] if c == 0 else ref.at[c, :, q1]
 
+    barrier = pltpu.get_barrier_semaphore()
+    for axis in range(2):
+        for d in range(2):
+            pl.semaphore_signal(barrier, inc=1, device_id={"dp": neighbour(axis, d)}, device_id_type=MESH)
+    pl.semaphore_wait(barrier, 4)
+
+    def slot(c, d, p, s):
+        return out_big[d].at[c * n + s] if p == 0 else od.at[c * n + s, d]
+
+    def send(src, dst, axis, d, p, sem):
+        sems = send_big if p == 0 else send_small
+        link = 2 * axis + d
+        pltpu.make_async_remote_copy(
+            src_ref=src, dst_ref=dst, send_sem=sems.at[link if p == 0 else axis], recv_sem=sem,
+            device_id={"dp": neighbour(axis, d)}, device_id_type=MESH).start()
+
+    def arrived(ref, sem):
+        pltpu.make_async_copy(ref, ref, sem).wait()
+
+    def to_slot(src, c, d, axis, p, s):
+        send(src, slot(c, d, p, s), axis, d, p, recv.at[c, d, p, s])
+
+    def wait_slot(c, d, p, s):
+        arrived(slot(c, d, p, s), recv.at[c, d, p, s])
+
+    def term_ref(c, h, p, q1, q2):
+        i, j = (q1, q2) if c == 0 else (q2, q1)
+        return g_big[h].at[c, i, j] if p == 0 else gd.at[c, i, j, h]
+
+    ks = (2, 1, -1, 0)
+
+    def step1(c, d, k):
+        for p in range(2):
+            to_slot(term_ref(c, d, p, near(at[c], 2), near(at[1 - c], ks[k])), c, d, c, p, k)
+
+    def step2(c, d, k):
+        for p in range(2):
+            to_slot(term_ref(c, 1 - d, p, near(at[c], SIGN[d]), near(at[1 - c], ks[k])), c, d, c, p, 4 + k)
+
+    for k in range(4):
+        for d in range(2):
+            for c in range(2):
+                step1(c, d, k)
+    for k in range(2):
+        for d in range(2):
+            for c in range(2):
+                step2(c, d, k)
+
     index = 0
     for d in range(2):
         for c in range(2):
@@ -124,53 +172,6 @@
             load(("own", c, h, 1), index + 1, (gd.at[c, at[c], :, h] if c == 0 else gd.at[c, :, at[c], h]), own_small.at[c, h])
             index += 2
 
-    barrier = pltpu.get_barrier_semaphore()
-    for i in range(1, n):
-        pl.semaphore_signal(barrier, inc=1, device_id={"dp": lax.rem(me + i, n)}, device_id_type=MESH)
-    pl.semaphore_wait(barrier, n - 1)
-
-    def slot(c, d, p, s):
-        return out_big[d].at[c * n + s] if p == 0 else od.at[c * n + s, d]
-
-    def send(src, dst, axis, d, p, sem):
-        sems = send_big if p == 0 else send_small
-        link = 2 * axis + d
-        pltpu.make_async_remote_copy(
-            src_ref=src, dst_ref=dst, send_sem=sems.at[link if p == 0 else axis], recv_sem=sem,
-            device_id={"dp": neighbour(axis, d)}, device_id_type=MESH).start()
-
-    def arrived(ref, sem):
-        pltpu.make_async_copy(ref, ref, sem).wait()
-
-    def to_slot(src, c, d, axis, p, s):
-        send(src, slot(c, d, p, s), axis, d, p, recv.at[c, d, p, s])
-
-    def wait_slot(c, d, p, s):
-        arrived(slot(c, d, p, s), recv.at[c, d, p, s])
-
-    def term_ref(c, h, p, q1, q2):
-        i, j = (q1, q2) if c == 0 else (q2, q1)
-        return g_big[h].at[c, i, j] if p == 0 else gd.at[c, i, j, h]
-
-    ks = (2, 1, -1, 0)
-
-    def step1(c, d, k):
-        for p in range(2):
-            to_slot(term_ref(c, d, p, near(at[c], 2), near(at[1 - c], ks[k])), c, d, c, p, k)
-
-    def step2(c, d, k):
-        for p in range(2):
-            to_slot(term_ref(c, 1 - d, p, near(at[c], SIGN[d]), near(at[1 - c], ks[k])), c, d, c, p, 4 + k)
-
-    for k in range(4):
-        for d in range(2):
-            for c in range(2):
-                step1(c, d, k)
-    for k in range(2):
-        for d in range(2):
-            for c in range(2):
-                step2(c, d, k)
-
     own = (own_big, own_small)
     fwd = (fwd_big, fwd_small)
     acc = (acc_big, acc_small)
@@ -266,10 +267,16 @@
 
     wait_sends()
 
-    part[me] = total
+    part[me] = jnp.sum(total, axis=0, keepdims=True)
     copies = []
-    for i in range(1, n):
-        to = lax.rem(me + i, n)
+    def far(i):
+        return sum(min(k, side - k) for k in (i // side, i % side))
+
+    def shifted(i, sign):
+        return near(at[0], sign * (i // side)) * side + near(at[1], sign * (i % side))
+
+    for i in sorted(range(1, n), key=far, reverse=True):
+        to = shifted(i, 1)
         copy = pltpu.make_async_remote_copy(
             src_ref=part.at[me], dst_ref=part.at[me], send_sem=part_send.at[i - 1], recv_sem=part_recv.at[i - 1],
             device_id={"dp": to}, device_id_type=MESH)
@@ -278,7 +285,7 @@
     for copy in list(loads.values())[16:]:
         copy.wait()
     for i in range(1, n):
-        back = lax.rem(me - i + n, n)
+        back = shifted(i, -1)
         arrived(part.at[back], part_recv.at[i - 1])
     total = part[0]
     for i in range(1, n):
@@ -328,8 +335,8 @@
 
 
 def write_out(*refs):
-    sem = refs[-1]
-    copies = [pltpu.make_async_copy(refs[i], refs[9 + i], sem.at[i]) for i in range(9)]
+    many = len(refs) // 2
+    copies = [pltpu.make_async_copy(refs[i], refs[many + i], refs[-1].at[i]) for i in range(many)]
     for copy in copies:
         copy.start()
     for copy in copies:
@@ -367,7 +374,7 @@
                 pltpu.VMEM((layers, 2, *small), F32),
                 pltpu.VMEM((2, layers, *big), BF16),
                 pltpu.VMEM((layers, 2, *small), BF16),
-                pltpu.VMEM((n, 8, 128), F32),
+                pltpu.VMEM((n, 1, 128), F32),
                 pltpu.SemaphoreType.DMA((25,)),
                 pltpu.SemaphoreType.DMA((4,)),
                 pltpu.SemaphoreType.DMA((2,)),

time: 277 us -> 275 us (level)
  no operation moved by 1% of the time
where the time goes in v2:
time: 275 us
  Pallas kernels  274 us (100%)
    pallas_call x1, Pallas kernels, step(): pl.pallas_call(functools.partial(kernel, n, side, count), out_shape=[pltp...  264 us
    pallas_call x1, Pallas kernels, step(): pl.pallas_call(write_out, out_shape=[jax.ShapeDtypeStruct(*one) for one i...  10.3 us

profile of v2, /device:TPU:96, one launch (start us, length us, event | category | flops | bytes accessed | tf_op | source)
XLA Modules:
  0.0 275.1 jit_solution(2980992652994204561)
XLA Ops:
  0.6 264.1 %shard_map.187 = (bf16[32,56,2304]{2,1,0:T(8,128)(2,1)S(1)}, bf16[32,56,2304]{2,1,0:T(8,128)(2,1)S(1)}, bf16[32,2,72,896]{3,2,1,0:T(8,128)(2,1)S(1)}, f32[2,56,2...) custom-call(bf16[2,4,4,56,2304]{4,3,2,1,0:T(8,128)(2,1)} %bitcast.13, ...), custom_call_target="tpu_custom_call" | custom-call | tf_op jit(solution)/shard_map/pallas_call | solution.py:363
  264.8 10.3 %shard_map.188 = (bf16[32,56,2304]{2,1,0:T(8,128)(2,1)}, bf16[32,56,2304]{2,1,0:T(8,128)(2,1)}, bf16[32,2,72,896]{3,2,1,0:T(8,128)(2,1)}, f32[2,56,2304]{2,1,0:T...) custom-call(bf16[32,56,2304]{2,1,0:T(8,128)(2,1)S(1)} %get-tuple-ele, ...), custom_call_target="tpu_custom_call" | custom-call | tf_op jit(solution)/shard_map/pallas_call | solution.py:387

commit v3 on v2

--- a/solution.py
+++ b/solution.py
@@ -116,6 +116,10 @@
         for d in range(2):
             pl.semaphore_signal(barrier, inc=1, device_id={"dp": neighbour(axis, d)}, device_id_type=MESH)
     pl.semaphore_wait(barrier, 4)
+
+    @pl.when(lax.rem(lax.axis_index("rep"), 2) == 0)
+    def _():
+        pl.delay(8000)
 
     def slot(c, d, p, s):
         return out_big[d].at[c * n + s] if p == 0 else od.at[c * n + s, d]

time: 275 us -> 270 us (0.982)
  Pallas kernels: 274 us -> 269 us
    pallas_call x1, Pallas kernels: 264 us -> 259 us  [step(): pl.pallas_call(functools.partial(kernel, n, side, count), out_shape=[pltp...]
where the time goes in v3:
time: 270 us
  Pallas kernels  269 us (100%)
    pallas_call x1, Pallas kernels, step(): pl.pallas_call(functools.partial(kernel, n, side, count), out_shape=[pltp...  259 us
    pallas_call x1, Pallas kernels, step(): pl.pallas_call(write_out, out_shape=[jax.ShapeDtypeStruct(*one) for one i...  10.3 us

profile of v3, /device:TPU:96, one launch (start us, length us, event | category | flops | bytes accessed | tf_op | source)
XLA Modules:
  0.0 269.5 jit_solution(5540880193313963269)
XLA Ops:
  0.6 258.6 %shard_map.187 = (bf16[32,56,2304]{2,1,0:T(8,128)(2,1)S(1)}, bf16[32,56,2304]{2,1,0:T(8,128)(2,1)S(1)}, bf16[32,2,72,896]{3,2,1,0:T(8,128)(2,1)S(1)}, f32[2,56,2...) custom-call(bf16[2,4,4,56,2304]{4,3,2,1,0:T(8,128)(2,1)} %bitcast.13, ...), custom_call_target="tpu_custom_call" | custom-call | tf_op jit(solution)/shard_map/pallas_call | solution.py:367
  259.3 10.3 %shard_map.188 = (bf16[32,56,2304]{2,1,0:T(8,128)(2,1)}, bf16[32,56,2304]{2,1,0:T(8,128)(2,1)}, bf16[32,2,72,896]{3,2,1,0:T(8,128)(2,1)}, f32[2,56,2304]{2,1,0:T...) custom-call(bf16[32,56,2304]{2,1,0:T(8,128)(2,1)S(1)} %get-tuple-ele, ...), custom_call_target="tpu_custom_call" | custom-call | tf_op jit(solution)/shard_map/pallas_call | solution.py:391

commit v4 on v3

--- a/solution.py
+++ b/solution.py
@@ -12,17 +12,37 @@
 F32, BF16 = jnp.float32, jnp.bfloat16
 MESH = pl.DeviceIdType.MESH
 SIGN = (1, -1)
-
-
-def gather_order(side):
+LAG_NS = 16000
+
+
+def next_device(me, side, axis, d):
+    at = (me // side, me % side)
+    moved = lax.rem(at[axis] + SIGN[d] + side, side)
+    return moved * side + at[1] if axis == 0 else at[0] * side + moved
+
+
+def meet(me, side):
+    barrier = pltpu.get_barrier_semaphore()
+    for axis in range(2):
+        for d in range(2):
+            pl.semaphore_signal(barrier, inc=1, device_id={"dp": next_device(me, side, axis, d)}, device_id_type=MESH)
+    pl.semaphore_wait(barrier, 4)
+
+
+def block_of(me, side, c, r1, r2):
+    at = (me // side, me % side)
+    q1, q2 = lax.rem(at[1 - c] + r1, side), lax.rem(at[c] + r2, side)
+    return q2 * side + q1 if c == 0 else q1 * side + q2
+
+
+def gather_order(side, part):
     free = {(a, d): 0.0 for a in range(2) for d in range(2)}
-    size = (2.0, 1.0)
     events, start, order, count = [], [], [], 0
 
     def enqueue(now, link, piece, d, first):
         nonlocal count
         c, r1, r2, h, p = piece
-        free[link] = max(free[link], now) + size[p]
+        free[link] = max(free[link], now) + 2.0
         there = (c, (r1 - SIGN[d]) % side, r2, h, p) if first else (c, r1, (r2 - SIGN[d]) % side, h, p)
         count += 1
         heapq.heappush(events, (free[link] + 1.0, count, there, link))
@@ -42,15 +62,14 @@
         return out
 
     now = 0.0
-    for p in (1, 0):
-        for h in range(2):
-            for c in range(2):
-                piece = (c, 0, 0, h, p)
-                todo = sends(piece, None)
-                start.append((piece, todo))
-                for a, d, first in todo:
-                    enqueue(now, (a, d), piece, d, first)
-                now += 0.1
+    for h in range(2):
+        for c in range(2):
+            piece = (c, 0, 0, h, part)
+            todo = sends(piece, None)
+            start.append((piece, todo))
+            for a, d, first in todo:
+                enqueue(now, (a, d), piece, d, first)
+            now += 0.1
     while events:
         now, _, piece, link = heapq.heappop(events)
         todo = sends(piece, link)
@@ -83,8 +102,8 @@
 
 
 def kernel(n, side, count, ga, gb, gd, wa, wb, wd, ma, mb, md, va, vb, vd,
-           oa, ob, od, oma, omb, omd, ova, ovb, ovd,
-           fwd_big, fwd_small, own_big, own_small, acc_big, acc_small, w_big, w_small, part,
+           oa, ob, mine_down, oma, omb, omd, ova, ovb, ovd,
+           od, fwd_big, fwd_small, own_big, own_small, acc_big, acc_small, w_big, w_small, part,
            load_sem, send_big, send_small, recv, part_send, part_recv):
     me = lax.axis_index("dp")
     at = (me // side, me % side)
@@ -93,8 +112,7 @@
         return q1 * side + q2 if c == 0 else q2 * side + q1
 
     def neighbour(axis, d):
-        moved = lax.rem(at[axis] + SIGN[d] + side, side)
-        return moved * side + at[1] if axis == 0 else at[0] * side + moved
+        return next_device(me, side, axis, d)
 
     def near(p, steps):
         return lax.rem(p + steps + side, side)
@@ -111,15 +129,11 @@
     def rows(ref, c, q1):
         return ref.at[c, q1] if c == 0 else ref.at[c, :, q1]
 
-    barrier = pltpu.get_barrier_semaphore()
-    for axis in range(2):
-        for d in range(2):
-            pl.semaphore_signal(barrier, inc=1, device_id={"dp": neighbour(axis, d)}, device_id_type=MESH)
-    pl.semaphore_wait(barrier, 4)
+    meet(me, side)
 
     @pl.when(lax.rem(lax.axis_index("rep"), 2) == 0)
     def _():
-        pl.delay(8000)
+        pl.delay(LAG_NS)
 
     def slot(c, d, p, s):
         return out_big[d].at[c * n + s] if p == 0 else od.at[c * n + s, d]
@@ -260,16 +274,18 @@
 
                 total = loop(shapes[p], body, total)
 
-    def wait_sends():
+    def wait_sends(parts):
         many = n - 1
-        for link in range(4):
-            ref = oa.at[pl.ds(0, many)]
-            pltpu.make_async_copy(ref, ref, send_big.at[link]).wait()
-        for axis in range(2):
-            ref = od.at[pl.ds(0, many)]
-            pltpu.make_async_copy(ref, ref, send_small.at[axis]).wait()
-
-    wait_sends()
+        if 0 in parts:
+            for link in range(4):
+                ref = oa.at[pl.ds(0, many)]
+                pltpu.make_async_copy(ref, ref, send_big.at[link]).wait()
+        if 1 in parts:
+            for axis in range(2):
+                ref = od.at[pl.ds(0, many)]
+                pltpu.make_async_copy(ref, ref, send_small.at[axis]).wait()
+
+    wait_sends((0, 1))
 
     part[me] = jnp.sum(total, axis=0, keepdims=True)
     copies = []
@@ -298,27 +314,20 @@
     factor = jnp.minimum(1.0, 0.5 * lax.rsqrt(total / count + 1e-30))
 
     oms, ovs = (oma, omb), (ova, ovb)
-    start, order = gather_order(side)
+    start, order = gather_order(side, 0)
 
     def gathered(piece):
-        c, r1, r2, h, p = piece
-        q1, q2 = near(at[1 - c], r1), near(at[c], r2)
-        b = q2 * side + q1 if c == 0 else q1 * side + q2
-        return (out_big[h].at[c * n + b] if p == 0 else od.at[c * n + b, h]), recv.at[c, h, p, b]
+        c, r1, r2, h, _ = piece
+        b = block_of(me, side, c, r1, r2)
+        return out_big[h].at[c * n + b], recv.at[c, h, 0, b]
 
     def pass_on(piece, todo):
         ref, sem = gathered(piece)
         for a, d, _ in todo:
-            send(ref, ref, a, d, piece[-1], sem)
-
-    for piece, todo in start:
-        c, _, _, h, p = piece
-        g = acc[p].at[c, h]
-        m, v = (oms[h].at[c], ovs[h].at[c]) if p == 0 else (omd.at[c, h], ovd.at[c, h])
-        w = w_big.at[h, c] if p == 0 else w_small.at[c, h]
-        out, _ = gathered(piece)
-
-        def body(cols, _, g=g, m=m, v=v, w=w, out=out):
+            send(ref, ref, a, d, 0, sem)
+
+    def take_step(g, m, v, w, out):
+        def body(cols, _):
             x = g[:, cols] * factor
             m1 = 0.9 * m[:, cols] + 0.1 * x
             v1 = 0.95 * v[:, cols] + 0.05 * x * x
@@ -328,21 +337,59 @@
             out[:, cols] = (w1 - 0.02 * (m1 * lax.rsqrt(v1 + 1e-8) + 0.1 * w1)).astype(BF16)
             return 0
 
-        loop(shapes[p], body)
+        loop(g.shape, body)
+
+    for piece, todo in start:
+        c, _, _, h, _ = piece
+        take_step(acc_big.at[c, h], oms[h].at[c], ovs[h].at[c], w_big.at[h, c], gathered(piece)[0])
         pass_on(piece, todo)
+    for c in range(2):
+        for h in range(2):
+            take_step(acc_small.at[c, h], omd.at[c, h], ovd.at[c, h], w_small.at[c, h], mine_down.at[c, h])
     for piece, todo in order:
         arrived(*gathered(piece))
         pass_on(piece, todo)
-    wait_sends()
+    wait_sends((0,))
     for copy in copies:
         copy.wait_send()
 
 
-def write_out(*refs):
-    many = len(refs) // 2
+def gather_down(n, side, mine, after, out, send_sem, recv):
+    me = lax.axis_index("dp")
+    meet(me, side)
+    start, order = gather_order(side, 1)
+
+    def gathered(piece):
+        c, r1, r2, h, _ = piece
+        b = block_of(me, side, c, r1, r2)
+        return out.at[c * n + b, h], recv.at[c, h, b]
+
+    def pass_on(piece, todo, src=None):
+        ref, sem = gathered(piece)
+        for a, d, _ in todo:
+            pltpu.make_async_remote_copy(
+                src_ref=ref if src is None else src, dst_ref=ref, send_sem=send_sem.at[a], recv_sem=sem,
+                device_id={"dp": next_device(me, side, a, d)}, device_id_type=MESH).start()
+
+    for piece, todo in start:
+        pass_on(piece, todo, mine.at[piece[0], piece[3]])
+    for piece, _ in start:
+        gathered(piece)[0][...] = mine[piece[0], piece[3]]
+    for piece, todo in order:
+        ref, sem = gathered(piece)
+        pltpu.make_async_copy(ref, ref, sem).wait()
+        pass_on(piece, todo)
+    for axis in range(2):
+        ref = out.at[pl.ds(0, n - 1)]
+        pltpu.make_async_copy(ref, ref, send_sem.at[axis]).wait()
+
+
+def write_out(many, *refs):
     copies = [pltpu.make_async_copy(refs[i], refs[many + i], refs[-1].at[i]) for i in range(many)]
     for copy in copies:
         copy.start()
+    for ref in refs[2 * many : -1]:
+        ref[...] = jnp.zeros(ref.shape, F32)
     for copy in copies:
         copy.wait()
 
@@ -366,10 +413,11 @@
         count = n * sum(one.size for one in m)
         res = pl.pallas_call(
             functools.partial(kernel, n, side, count),
-            out_shape=[pltpu.VMEM(*one) for one in outs],
+            out_shape=[pltpu.VMEM(*one) for one in (*outs[:2], ((layers, 2, *small), BF16), *outs[3:])],
             in_specs=[pl.BlockSpec(memory_space=pl.ANY)] * 12,
             out_specs=[pl.BlockSpec(memory_space=pltpu.VMEM)] * 9,
             scratch_shapes=[
+                pltpu.VMEM(*outs[2]),
                 pltpu.VMEM((layers, 2, side, *big), BF16),
                 pltpu.VMEM((layers, 2, side, *small), BF16),
                 pltpu.VMEM((layers, 2, side, *big), BF16),
@@ -386,16 +434,28 @@
                 pltpu.SemaphoreType.DMA((n - 1,)),
                 pltpu.SemaphoreType.DMA((n - 1,)),
             ],
-            compiler_params=pltpu.CompilerParams(collective_id=0, has_side_effects=True, vmem_limit_bytes=24 * 2**20),
+            compiler_params=pltpu.CompilerParams(collective_id=0, has_side_effects=True, vmem_limit_bytes=32 * 2**20),
         )(*ins)
-        res = pl.pallas_call(
-            write_out,
-            out_shape=[jax.ShapeDtypeStruct(*one) for one in outs],
-            in_specs=[pl.BlockSpec(memory_space=pltpu.VMEM)] * 9,
-            out_specs=[pl.BlockSpec(memory_space=pl.ANY)] * 9,
-            scratch_shapes=[pltpu.SemaphoreType.DMA((9,))],
-            compiler_params=pltpu.CompilerParams(vmem_limit_bytes=2**20),
-        )(*res)
+        def write(arrays, more):
+            return pl.pallas_call(
+                functools.partial(write_out, len(arrays)),
+                out_shape=[*(jax.ShapeDtypeStruct(one.shape, one.dtype) for one in arrays), *[jax.ShapeDtypeStruct((8, 128), F32)] * more],
+                in_specs=[pl.BlockSpec(memory_space=pltpu.VMEM)] * len(arrays),
+                out_specs=[pl.BlockSpec(memory_space=pl.ANY)] * len(arrays) + [pl.BlockSpec(memory_space=pltpu.VMEM)] * more,
+                scratch_shapes=[pltpu.SemaphoreType.DMA((len(arrays),))],
+                compiler_params=pltpu.CompilerParams(vmem_limit_bytes=2**20),
+            )(*arrays)
+
+        written = write([*res[:2], *res[3:]], 1)
+        down = pl.pallas_call(
+            functools.partial(gather_down, n, side),
+            out_shape=pltpu.VMEM(*outs[2]),
+            in_specs=[pl.BlockSpec(memory_space=pltpu.VMEM), pl.BlockSpec(memory_space=pl.ANY)],
+            out_specs=pl.BlockSpec(memory_space=pltpu.VMEM),
+            scratch_shapes=[pltpu.SemaphoreType.DMA((2,)), pltpu.SemaphoreType.DMA((layers, 2, n))],
+            compiler_params=pltpu.CompilerParams(collective_id=1, has_side_effects=True, vmem_limit_bytes=2 * 2**20),
+        )(res[2], written[-1])
+        res = [*written[:2], write([down], 0)[0], *written[2:-1]]
         return tuple(r.reshape(layers, -1, r.shape[-1]) for r in res)
 
     all_of, cut = P(None, None, None), P(None, "dp", None)

time: 270 us -> 264 us (0.978)
  Pallas kernels: 269 us -> 264 us
    pallas_call x1, Pallas kernels: 259 us -> 221 us  [step(): pl.pallas_call(functools.partial(kernel, n, side, count), out_shape=[pltp...]
    pallas_call x1 -> x3, Pallas kernels: 10.3 us -> 42.4 us  [the longest x1 31.3 us: step(): pl.pallas_call(functools.partial(gather_down, n, side), out_shape=pltpu.V...]
where the time goes in v4:
time: 264 us
  Pallas kernels  264 us (100%)
    pallas_call x1, Pallas kernels, step(): pl.pallas_call(functools.partial(kernel, n, side, count), out_shape=[pltp...  221 us
    pallas_call x1, Pallas kernels, step(): pl.pallas_call(functools.partial(gather_down, n, side), out_shape=pltpu.V...  31.3 us
    pallas_call x2, Pallas kernels, write(): pl.pallas_call(functools.partial(write_out, len(arrays)), out_shape=[*(ja...  11.1 us

profile of v4, /device:TPU:96, one launch (start us, length us, event | category | flops | bytes accessed | tf_op | source)
XLA Modules:
  0.0 264.3 jit_solution(11680679285984796221)
XLA Ops:
  0.6 221.2 %shard_map.187 = (bf16[32,56,2304]{2,1,0:T(8,128)(2,1)S(1)}, bf16[32,56,2304]{2,1,0:T(8,128)(2,1)S(1)}, bf16[2,2,72,896]{3,2,1,0:T(8,128)(2,1)S(1)}, f32[2,56,23...) custom-call(bf16[2,4,4,56,2304]{4,3,2,1,0:T(8,128)(2,1)} %bitcast.14, ...), custom_call_target="tpu_custom_call" | custom-call | tf_op jit(solution)/shard_map/pallas_call | solution.py:414
  221.9 7.8 %shard_map.188 = (bf16[32,56,2304]{2,1,0:T(8,128)(2,1)}, bf16[32,56,2304]{2,1,0:T(8,128)(2,1)}, f32[2,56,2304]{2,1,0:T(8,128)}, f32[2,56,2304]{2,1,0:T(8,128)}, ...) custom-call(bf16[32,56,2304]{2,1,0:T(8,128)(2,1)S(1)} %get-tuple-ele, ...), custom_call_target="tpu_custom_call" | custom-call | tf_op jit(solution)/shard_map/pallas_call | solution.py:440
  229.7 31.3 %shard_map.189.refs_0_ = bf16[32,2,72,896]{3,2,1,0:T(8,128)(2,1)S(1)} custom-call(bf16[2,2,72,896]{3,2,1,0:T(8,128)(2,1)S(1)} %get-tuple-element.37.mine, f32[8,128]{1,0:T(8,128)S(1)} %get-tuple-element.38.after), custom_call_target="tpu_custom_call" | custom-call | tf_op jit(solution)/shard_map/pallas_call | solution.py:450
  261.0 3.4 %shard_map.190 = bf16[32,2,72,896]{3,2,1,0:T(8,128)(2,1)} custom-call(bf16[32,2,72,896]{3,2,1,0:T(8,128)(2,1)S(1)} %shard_map.189.refs_0_), custom_call_target="tpu_custom_call" | custom-call | tf_op jit(solution)/shard_map/pallas_call | solution.py:440

commit v5 on v4

--- a/solution.py
+++ b/solution.py
@@ -64,12 +64,14 @@
     now = 0.0
     for h in range(2):
         for c in range(2):
-            piece = (c, 0, 0, h, part)
-            todo = sends(piece, None)
-            start.append((piece, todo))
-            for a, d, first in todo:
-                enqueue(now, (a, d), piece, d, first)
-            now += 0.1
+            start.append(((c, 0, 0, h, part), sends((c, 0, 0, h, part), None)))
+    if part == 1:
+        start = [(piece, [one for one in todo if (one[1] == piece[3]) == now]) for now in (True, False) for piece, todo in start]
+    now = 0.0
+    for piece, todo in start:
+        for a, d, first in todo:
+            enqueue(now, (a, d), piece, d, first)
+        now += 0.1
     while events:
         now, _, piece, link = heapq.heappop(events)
         todo = sends(piece, link)
@@ -373,7 +375,7 @@
 
     for piece, todo in start:
         pass_on(piece, todo, mine.at[piece[0], piece[3]])
-    for piece, _ in start:
+    for piece in dict.fromkeys(piece for piece, _ in start):
         gathered(piece)[0][...] = mine[piece[0], piece[3]]
     for piece, todo in order:
         ref, sem = gathered(piece)

time: 264 us -> 263 us (level)
  no operation moved by 1% of the time
where the time goes in v5:
time: 263 us; the launch traced here: 262 us
  Pallas kernels  262 us (100%)
    pallas_call x1, Pallas kernels, step(): pl.pallas_call(functools.partial(kernel, n, side, count), out_shape=[pltp...  221 us
    pallas_call x1, Pallas kernels, step(): pl.pallas_call(functools.partial(gather_down, n, side), out_shape=pltpu.V...  29.4 us
    pallas_call x2, Pallas kernels, write(): pl.pallas_call(functools.partial(write_out, len(arrays)), out_shape=[*(ja...  11.1 us

profile of v5, /device:TPU:96, one launch (start us, length us, event | category | flops | bytes accessed | tf_op | source)
XLA Modules:
  0.0 262.4 jit_solution(16982968117342157149)
XLA Ops:
  0.6 221.2 %shard_map.187 = (bf16[32,56,2304]{2,1,0:T(8,128)(2,1)S(1)}, bf16[32,56,2304]{2,1,0:T(8,128)(2,1)S(1)}, bf16[2,2,72,896]{3,2,1,0:T(8,128)(2,1)S(1)}, f32[2,56,23...) custom-call(bf16[2,4,4,56,2304]{4,3,2,1,0:T(8,128)(2,1)} %bitcast.14, ...), custom_call_target="tpu_custom_call" | custom-call | tf_op jit(solution)/shard_map/pallas_call | solution.py:416
  221.9 7.8 %shard_map.188 = (bf16[32,56,2304]{2,1,0:T(8,128)(2,1)}, bf16[32,56,2304]{2,1,0:T(8,128)(2,1)}, f32[2,56,2304]{2,1,0:T(8,128)}, f32[2,56,2304]{2,1,0:T(8,128)}, ...) custom-call(bf16[32,56,2304]{2,1,0:T(8,128)(2,1)S(1)} %get-tuple-ele, ...), custom_call_target="tpu_custom_call" | custom-call | tf_op jit(solution)/shard_map/pallas_call | solution.py:442
  229.7 29.4 %shard_map.189.refs_0_ = bf16[32,2,72,896]{3,2,1,0:T(8,128)(2,1)S(1)} custom-call(bf16[2,2,72,896]{3,2,1,0:T(8,128)(2,1)S(1)} %get-tuple-element.37.mine, f32[8,128]{1,0:T(8,128)S(1)} %get-tuple-element.38.after), custom_call_target="tpu_custom_call" | custom-call | tf_op jit(solution)/shard_map/pallas_call | solution.py:452
  259.1 3.4 %shard_map.190 = bf16[32,2,72,896]{3,2,1,0:T(8,128)(2,1)} custom-call(bf16[32,2,72,896]{3,2,1,0:T(8,128)(2,1)S(1)} %shard_map.189.refs_0_), custom_call_target="tpu_custom_call" | custom-call | tf_op jit(solution)/shard_map/pallas_call | solution.py:442
